TPU v7x, 128 devices: a whole 4x4x4 slice. The times are simulated.
128 devices in a mesh: gx: 8 (over z, core), gy: 16 (over x, y).
Axes of the slice: x: 4, y: 4, z: 4, core: 2. Of those that a mesh axis runs over, the one named last changes fastest.
Arguments:
- vorticity: float32 [8192, 8192], P('gx', 'gy'), may hold values from -6 to 6
- tile_list: int32 [128, 64], P(('gx', 'gy')), may hold values from 0 to 4095, as said below
- float_slot: int32 [262144], P(('gx', 'gy')), may hold values from 0 to 63, as said below
- float_cell: int32 [2, 262144], P(None, ('gx', 'gy')), may hold values from 1 to 125
- float_frac: float32 [2, 262144], P(None, ('gx', 'gy')), may hold values from 0 to 1
Outputs:
- float_velocity: float32 [2, 262144], P(None, ('gx', 'gy'))
Inputs may be any that keep to these rules, and one draw needn't show every extreme that they name: `tile_list`: row b lists the 64 tiles used by float block b; tile t covers the 128 x 128 cells from row (t // 64) * 128 and column (t % 64) * 128. The 64 tiles of a row lie in the blocks of vorticity held by 64 different devices, and one device's block is named by every row. `float_slot`: at most 64 floats of one block name the same position; in every block the position whose tile lies in the device block named by every row of tile_list is named by exactly 64 floats.
All inputs are finite; a program needn't handle non-finite values.
Results may differ from a plain program's by a relative error of at most 0.0031.
Values may be sent and summed in bfloat16 or wider, within the bound.
No kernel may reach another device: no remote copies, remote signals or barrier semaphores. Data moves between devices by JAX's collectives and lax.ppermute only.
A program may use at most 128 MiB of HBM per device.

v0:
```python
import functools
import math

import jax
import jax.numpy as jnp
import numpy as np
from jax import lax
from jax.experimental import pallas as pl
from jax.experimental.pallas import tpu as pltpu
from jax.sharding import PartitionSpec as P

N = 8192
KAPPA = math.pi / N
BF = jnp.bfloat16
F32 = jnp.float32
VMEM = 60 * 1024 * 1024


def _mul_const(v, c, s):
    re, im = v
    if abs(s) < 1e-12:
        if abs(c - 1.0) < 1e-12:
            return v
        if abs(c + 1.0) < 1e-12:
            return _sub((None, None), v)
    if abs(c) < 1e-12:
        return _times_i(v, s)
    if re is None:
        return (im * -s, im * c)
    if im is None:
        return (re * c, re * s)
    if abs(abs(c) - abs(s)) < 1e-12:
        q = abs(c)
        a, b = (1 if c > 0 else -1), (1 if s > 0 else -1)
        if a == b:
            return ((re - im) * (q * a), (re + im) * (q * a))
        return ((re + im) * (q * a), (im - re) * (q * a))
    return (re * c - im * s, re * s + im * c)


def _add(x, y):
    def one(p, q):
        if p is None:
            return q
        return p if q is None else p + q

    return (one(x[0], y[0]), one(x[1], y[1]))


def _sub(x, y):
    def one(p, q):
        if q is None:
            return p
        return -q if p is None else p - q

    return (one(x[0], y[0]), one(x[1], y[1]))


def _times_i(v, sign):
    re, im = v
    if sign > 0:
        return (None if im is None else -im, re)
    return (im, None if re is None else -re)


def fft_list(xs, sign):
    n = len(xs)
    if n == 1:
        return xs
    if n == 2:
        return [_add(xs[0], xs[1]), _sub(xs[0], xs[1])]
    if n == 4:
        s, d = _add(xs[0], xs[2]), _sub(xs[0], xs[2])
        t, e = _add(xs[1], xs[3]), _times_i(_sub(xs[1], xs[3]), sign)
        return [_add(s, t), _add(d, e), _sub(s, t), _sub(d, e)]
    outer = 4 if n % 4 == 0 and n > 8 else 2
    inner = n // outer
    cols = [fft_list(xs[j::outer], sign) for j in range(outer)]
    out = [None] * n
    for k0 in range(inner):
        row = []
        for j in range(outer):
            ang = sign * 2.0 * math.pi * j * k0 / n
            row.append(_mul_const(cols[j][k0], math.cos(ang), math.sin(ang)))
        for k1, v in enumerate(fft_list(row, sign)):
            out[k0 + inner * k1] = v
    return out


def split2(x):
    hi = x.astype(BF)
    return hi, (x - hi.astype(F32)).astype(BF)


def table_split(t):
    t = np.asarray(t, np.float64)
    hi = t.astype(np.float32).astype(jnp.bfloat16)
    lo = (t - hi.astype(np.float64)).astype(np.float32).astype(jnp.bfloat16)
    return hi, lo


def mm(a, b):
    return lax.dot_general(a, b, (((1,), (0,)), ((), ())), preferred_element_type=F32)


def mm_nt(a, b):
    return lax.dot_general(a, b, (((1,), (1,)), ((), ())), preferred_element_type=F32)


def mm_tn(a, b):
    return lax.dot_general(a, b, (((0,), (0,)), ((), ())), preferred_element_type=F32)


def call(kernel, out_shape, scratch, *args, specs=None):
    params = dict(
        out_shape=out_shape,
        scratch_shapes=scratch,
        compiler_params=pltpu.CompilerParams(vmem_limit_bytes=VMEM),
    )
    if specs is not None:
        params["in_specs"] = specs
    return pl.pallas_call(kernel, **params)(*args)


def cast_kernel(x_ref, o_ref):
    s = lax.broadcasted_iota(jnp.int32, (8, 8, 128), 1)

    def handed(x, rows, shift):
        error = jnp.where(rows, x.astype(BF).astype(F32) - x, 0.0)
        return x - pltpu.roll(error, shift, 1)

    for q in range(4):
        x = x_ref[:, q * 128 : (q + 1) * 128].reshape(8, 8, 128)
        x = handed(x, s % 2 == 0, 1)
        x = handed(x, s % 4 == 1, 2)
        o_ref[0, q] = x.reshape(64, 128).astype(BF)


def cast_block(vorticity):
    return pl.pallas_call(
        cast_kernel,
        grid=(16,),
        in_specs=[pl.BlockSpec((64, 512), lambda i: (i, 0))],
        out_specs=pl.BlockSpec((1, 4, 64, 128), lambda i: (i, 0, 0, 0)),
        out_shape=jax.ShapeDtypeStruct((16, 4, 64, 128), BF),
    )(vorticity)


def rows_kernel(x_ref, twr_ref, twi_ref, thi_ref, tlo_ref, alt_ref, o_ref, a_ref, yhi_ref, ylo_ref):
    def first(t, carry):
        rows = pl.ds(pl.multiple_of(t * 16, 16), 16)
        for j in range(8):
            xs = [(x_ref[8 * i + j, rows, :].astype(F32), None) for i in range(8)]
            ys = fft_list(xs, -1.0)
            for k0 in range(5):
                ang = -2.0 * math.pi * j * k0 / 64
                re, im = _mul_const(ys[k0], math.cos(ang), math.sin(ang))
                zero = jnp.zeros((16, 128), F32)
                a_ref[k0, j, 0, rows, :] = zero if re is None else re
                a_ref[k0, j, 1, rows, :] = zero if im is None else im
        return carry

    lax.fori_loop(0, 4, first, 0)

    def put(k, re, im, rows):
        cr, ci = twr_ref[k], twi_ref[k]
        yr, yi = re * cr - im * ci, re * ci + im * cr
        hr, lr = split2(yr)
        hi, li = split2(yi)
        yhi_ref[k, rows, 0:128] = hr
        yhi_ref[k, rows, 128:256] = hi
        ylo_ref[k, rows, 0:128] = lr
        ylo_ref[k, rows, 128:256] = li

    def second(t, carry):
        rows = pl.ds(pl.multiple_of(t * 16, 16), 16)
        for k0 in range(5):
            zs = fft_list([(a_ref[k0, j, 0, rows, :], a_ref[k0, j, 1, rows, :]) for j in range(8)], -1.0)
            for k1 in range(8):
                k = k0 + 8 * k1
                re, im = zs[k1]
                put(k, re, im, rows)
                if k0 in (1, 2, 3):
                    put(64 - k, re, -im, rows)
        return carry

    lax.fori_loop(0, 4, second, 0)

    def third(kap, carry):
        yhi = yhi_ref[pl.ds(2 * kap, 2)].reshape(128, 256)
        ylo = ylo_ref[pl.ds(2 * kap, 2)].reshape(128, 256)
        z = mm_nt(thi_ref[...], yhi) + mm_nt(tlo_ref[...], yhi) + mm_nt(thi_ref[...], ylo)
        zb = z.astype(BF)
        for g in range(4):
            for c in range(2):
                o_ref[4 * kap + g, c] = zb[c * 64 + 16 * g : c * 64 + 16 * g + 16, :]
        return carry

    lax.fori_loop(0, 32, third, 0)

    nyq = mm_nt(alt_ref[...], yhi_ref[0:2].reshape(128, 256)) + mm_nt(
        alt_ref[...], ylo_ref[0:2].reshape(128, 256)
    )
    lane = lax.broadcasted_iota(jnp.int32, (16, 128), 1)
    sub = lax.broadcasted_iota(jnp.int32, (16, 128), 0)
    old = o_ref[0, 1].astype(F32)
    o_ref[0, 1] = jnp.where((lane < 64) & (sub == 0), nyq, old).astype(BF)


@functools.cache
def rows_tables():
    k = np.arange(64)[:, None, None]
    b = np.arange(128)[None, None, :]
    tw = np.exp(-2j * np.pi * k * b / N)
    w = np.exp(-2j * np.pi * np.arange(64)[:, None] * np.arange(128)[None, :] / 128)
    t = np.block([[w.real, -w.imag], [w.imag, w.real]])
    alt = np.zeros((16, 256))
    alt[0, :128] = (-1.0) ** np.arange(128)
    hi, lo = table_split(t)
    return (
        tw.real.astype(np.float32),
        tw.imag.astype(np.float32),
        hi,
        lo,
        alt.astype(np.float32).astype(jnp.bfloat16),
    )


def rows_forward(x):
    return call(
        rows_kernel,
        jax.ShapeDtypeStruct((128, 2, 16, 128), BF),
        [
            pltpu.VMEM((5, 8, 2, 64, 128), F32),
            pltpu.VMEM((64, 64, 256), BF),
            pltpu.VMEM((64, 64, 256), BF),
        ],
        x,
        *rows_tables(),
    )


def fft128(load, store, a_ref, rows, sign):
    for j in range(8):
        ys = fft_list([load(8 * i + j) for i in range(16)], sign)
        for k0 in range(16):
            ang = sign * 2.0 * math.pi * j * k0 / 128
            re, im = _mul_const(ys[k0], math.cos(ang), math.sin(ang))
            a_ref[k0, j, 0, rows, :] = re
            a_ref[k0, j, 1, rows, :] = im
    for k0 in range(16):
        zs = fft_list([(a_ref[k0, j, 0, rows, :], a_ref[k0, j, 1, rows, :]) for j in range(8)], sign)
        for k1 in range(8):
            store(k0 + 16 * k1, zs[k1])


def cols_kernel(
    x_ref, twr_ref, twi_ref, tw2r_ref, tw2i_ref, fhi_ref, flo_ref, bhi_ref, blo_ref,
    wm2_ref, pm_ref, sm_ref, del_ref, wn2_ref, pn_ref, sn_ref, hm_ref,
    o_ref,
    x32_ref, a_ref, yhi_ref, ylo_ref, e_ref, ce_ref, z_ref, shi_ref, slo_ref, p_ref,
):
    def widen(t, carry):
        for u in range(8):
            x32_ref[8 * t + u] = x_ref[8 * t + u].astype(F32)
        return carry

    lax.fori_loop(0, 16, widen, 0)

    def forward(hh, carry):
        rows = pl.ds(pl.multiple_of(hh * 8, 8), 8)

        def store(k, v):
            re, im = v
            cr, ci = twr_ref[k], twi_ref[k]
            yr, yi = re * cr - im * ci, re * ci + im * cr
            x32_ref[k, 0, rows, :] = yr
            x32_ref[k, 1, rows, :] = yi

            @pl.when(hh == 0)
            def _():
                back = (128 - k) % 128
                e_ref[0, back : back + 1, :] = re[0:1, :]
                e_ref[1, back : back + 1, :] = -im[0:1, :]

        fft128(lambda d: (x32_ref[d, 0, rows, :], x32_ref[d, 1, rows, :]), store, a_ref, rows, -1.0)
        return carry

    lax.fori_loop(0, 2, forward, 0)

    def second_split(t, carry):
        for u in range(8):
            k = 8 * t + u
            rows = pl.ds(pl.multiple_of(k * 16, 16), 16)
            hr, lr = split2(x32_ref[k, 0])
            hi, li = split2(x32_ref[k, 1])
            yhi_ref[rows, 0:128] = hr
            yhi_ref[rows, 128:256] = hi
            ylo_ref[rows, 0:128] = lr
            ylo_ref[rows, 128:256] = li
        return carry

    lax.fori_loop(0, 16, second_split, 0)

    fhi, flo = fhi_ref[...], flo_ref[...]

    er, ei = e_ref[0], e_ref[1]
    cr, ci = tw2r_ref[...], tw2i_ref[...]
    e_r, e_i = er * cr - ei * ci, er * ci + ei * cr
    hr, lr = split2(e_r)
    hi, li = split2(e_i)
    ehi = jnp.concatenate([hr, hi], axis=1)
    elo = jnp.concatenate([lr, li], axis=1)
    ce = mm(ehi, fhi) + mm(elo, fhi) + mm(ehi, flo)
    ce_ref[0] = ce[:, 0:128]
    ce_ref[1] = ce[:, 128:256]

    def matmul_f(t, carry):
        rows = pl.ds(pl.multiple_of(t * 256, 256), 256)
        z_ref[rows, :] = mm(yhi_ref[rows, :], fhi) + mm(ylo_ref[rows, :], fhi) + mm(yhi_ref[rows, :], flo)
        return carry

    lax.fori_loop(0, 8, matmul_f, 0)

    wn2, pn, sn, hm = wn2_ref[...], pn_ref[...], sn_ref[...], hm_ref[...]

    def spectral(t, carry):
        for u in range(8):
            k = 8 * t + u
            rows = pl.ds(pl.multiple_of(k * 16, 16), 16)
            zr, zi = z_ref[rows, 0:128], z_ref[rows, 128:256]
            fac = 1.0 / ((wm2_ref[k] + wn2 + KAPPA * KAPPA) * (pm_ref[k] * pn))
            dd = del_ref[k] * hm
            fr = fac * zr + dd * (ce_ref[0, pl.ds(k, 1), :] - zr)
            fi = fac * zi + dd * (ce_ref[1, pl.ds(k, 1), :] - zi)
            sm = sm_ref[k]
            for f, (re, im) in enumerate(((-sm * fi, sm * fr), (sn * fi, -sn * fr))):
                hr, lr = split2(re)
                hi, li = split2(im)
                shi_ref[f, rows, 0:128] = hr
                shi_ref[f, rows, 128:256] = hi
                slo_ref[f, rows, 0:128] = lr
                slo_ref[f, rows, 128:256] = li
        return carry

    lax.fori_loop(0, 16, spectral, 0)

    bhi, blo = bhi_ref[...], blo_ref[...]

    for f in range(2):

        def matmul_b(t, carry):
            rows = pl.ds(pl.multiple_of(t * 256, 256), 256)
            hi, lo = shi_ref[f, rows, :], slo_ref[f, rows, :]
            p_ref[rows, :] = mm(hi, bhi) + mm(lo, bhi) + mm(hi, blo)
            return carry

        lax.fori_loop(0, 8, matmul_b, 0)

        def inverse(hh, carry):
            rows = pl.ds(pl.multiple_of(hh * 8, 8), 8)

            def load(k):
                at = pl.ds(pl.multiple_of(k * 16 + hh * 8, 8), 8)
                re, im = p_ref[at, 0:128], p_ref[at, 128:256]
                cr, ci = twr_ref[k], twi_ref[k]
                return (re * cr + im * ci, im * cr - re * ci)

            def store(k, v):
                x32_ref[k, 0, rows, :] = v[0]
                x32_ref[k, 1, rows, :] = v[1]

            fft128(load, store, a_ref, rows, 1.0)
            return carry

        lax.fori_loop(0, 2, inverse, 0)

        def narrow(t, carry):
            for u in range(8):
                o_ref[8 * t + u, f] = x32_ref[8 * t + u].astype(BF)
            return carry

        lax.fori_loop(0, 16, narrow, 0)


def _wave(j, length):
    signed = np.where(j < length // 2, j, j - length).astype(np.float64)
    return 2.0 * np.pi / length * signed


@functools.cache
def cols_tables():
    lane = np.arange(128)
    kk = np.arange(128)[:, None]
    tw = np.exp(-2j * np.pi * kk * (lane % 64)[None, :] / N)
    w = np.exp(-2j * np.pi * np.outer(np.arange(64), np.arange(64)) / 64)
    eye = np.eye(2)
    wr, wi = np.kron(eye, w.real), np.kron(eye, w.imag)
    forward = np.block([[wr, wi], [-wi, wr]])
    backward = np.block([[wr, -wi], [wi, wr]])
    m = kk + 128 * (lane % 64)[None, :]
    wm = _wave(m, N)
    sm = np.where(m == N // 2, 0.0, wm)
    pm = (2.0 + np.cos(wm)) / 3.0
    f0 = 1.0 / ((wm**2 + KAPPA**2) * pm * float(N) ** 2)
    f1 = 1.0 / ((wm**2 + math.pi**2 + KAPPA**2) * pm * (1.0 / 3.0) * float(N) ** 2)
    delta = (f0 - f1) / 2.0

    def three(t):
        return np.asarray(t, np.float32)[:, None, :]

    twr, twi = tw.real.astype(np.float32), tw.imag.astype(np.float32)
    return (
        (three(twr), three(twi), twr, twi, *table_split(forward), *table_split(backward)),
        (three(wm**2), three(pm), three(sm), three(delta)),
    )


def cols_step(x, device):
    first, second = cols_tables()
    h = lax.broadcasted_iota(jnp.int32, (16, 128), 0)
    p = lax.broadcasted_iota(jnp.int32, (16, 128), 1) // 64
    n = 2 * (device // 4) + p + 64 * (16 * (device % 4) + h)
    wn = (2.0 * math.pi / N) * n.astype(F32)
    pn = (2.0 + jnp.cos(wn)) / 3.0 * (float(N) ** 2)
    pn = jnp.where(n == 0, pn, pn * 0.5)
    hm = jnp.where(n == 0, 1.0, 0.0).astype(F32)
    return call(
        cols_kernel,
        jax.ShapeDtypeStruct((128, 2, 2, 16, 128), BF),
        [
            pltpu.VMEM((128, 2, 16, 128), F32),
            pltpu.VMEM((16, 8, 2, 16, 128), F32),
            pltpu.VMEM((2048, 256), BF),
            pltpu.VMEM((2048, 256), BF),
            pltpu.VMEM((2, 128, 128), F32),
            pltpu.VMEM((2, 128, 128), F32),
            pltpu.VMEM((2048, 256), F32),
            pltpu.VMEM((2, 2048, 256), BF),
            pltpu.VMEM((2, 2048, 256), BF),
            pltpu.VMEM((2048, 256), F32),
        ],
        x, *first, *second, wn * wn, pn, wn, hm,
    )


def back_kernel(x_ref, t_ref, t0r_ref, t0i_ref, omr_ref, omi_ref, alt_ref, o_ref, s_ref, f_ref):
    table = t_ref[...]

    def first(kap, carry):
        cols = []
        for f in range(2):
            re = x_ref[pl.ds(4 * kap, 4), f, 0].reshape(64, 128)
            im = x_ref[pl.ds(4 * kap, 4), f, 1].reshape(64, 128)
            cols.append(jnp.concatenate([re, im, re, im], axis=0))
        s_ref[kap] = mm(table, jnp.concatenate(cols, axis=1))
        return carry

    lax.fori_loop(0, 32, first, 0)

    row = x_ref[0, 0, 1].astype(F32)[0:1, :]
    lane = lax.broadcasted_iota(jnp.int32, (128, 128), 1)
    s_ref[0, 0:128, 0:128] += jnp.where(lane < 64, alt_ref[...] * row, 0.0)

    low = lax.broadcasted_iota(jnp.int32, (8, 128), 1) < 64

    def second(t, carry):
        at = pl.ds(pl.multiple_of(t * 8, 8), 8)
        ati = pl.ds(pl.multiple_of(128 + t * 8, 8), 8)
        omr, omi = omr_ref[at, :], omi_ref[at, :]
        for f in range(2):
            tr, ti = t0r_ref[at, :], t0i_ref[at, :]
            xs = []
            for kap in range(32):
                re = s_ref[kap, at, f * 128 : (f + 1) * 128]
                im = s_ref[kap, ati, f * 128 : (f + 1) * 128]
                xs.append((re * tr - im * ti, re * ti + im * tr))
                tr, ti = tr * omr - ti * omi, tr * omi + ti * omr
            ys = fft_list(xs, 1.0)
            ts = []
            for x1 in range(32):
                re, im = ys[x1]
                ang = 2.0 * math.pi * x1 / 64
                ts.append(jnp.where(low, re, re * math.cos(ang) - im * math.sin(ang)))
            for e in range(16):
                ta, tb = ts[2 * e], ts[2 * e + 1]
                even = jnp.where(low, ta, pltpu.roll(tb, 64, 1))
                odd = jnp.where(low, pltpu.roll(ta, 64, 1), tb)
                f_ref[e // 2, f, e % 2, at, :] = even + odd
                f_ref[e // 2 + 8, f, e % 2, at, :] = even - odd
        return carry

    lax.fori_loop(0, 16, second, 0)

    def narrow(j, carry):
        o_ref[j] = f_ref[j].astype(BF)
        return carry

    lax.fori_loop(0, 16, narrow, 0)


@functools.cache
def back_tables():
    x0 = np.arange(128)
    e = np.exp(2j * np.pi * np.outer(x0, np.arange(64)) / 128)
    t = np.block([[e.real, -e.imag], [e.imag, e.real]])
    hi, lo = table_split(t)
    p = np.arange(128)[None, :] // 64
    t0 = np.exp(2j * np.pi * p * x0[:, None] / N)
    om = np.exp(2j * np.pi * 2 * x0[:, None] / N) * np.ones((1, 128))
    alt = ((-1.0) ** x0)[:, None] * np.ones((1, 128))
    f = lambda v: np.ascontiguousarray(v, np.float32)
    return (np.concatenate([hi, lo], axis=1), f(t0.real), f(t0.imag), f(om.real), f(om.imag), f(alt))


def rows_back(x):
    return call(
        back_kernel,
        jax.ShapeDtypeStruct((16, 2, 2, 128, 128), BF),
        [pltpu.VMEM((32, 256, 256), F32), pltpu.VMEM((16, 2, 2, 128, 128), F32)],
        x,
        *back_tables(),
    )


def split3(x):
    hi = x.astype(BF)
    rest = x - hi.astype(F32)
    mid = rest.astype(BF)
    return hi, mid, (rest - mid.astype(F32)).astype(BF)


def plan_kernel(list_ref, slot_ref, cell_ref, frac_ref, tri_ref, msg_ref, own_ref, s_ref, r_ref):
    slot = slot_ref[...]
    pick = lax.broadcasted_iota(jnp.int32, (64, 2048), 0) == slot
    tile = jnp.sum(jnp.where(pick, list_ref[...], 0), axis=0, keepdims=True)
    grid_row, grid_col = tile // 64, tile % 64
    owner = (grid_row // 8) * 16 + grid_col // 4
    local = ((grid_row % 8) * 4 + grid_col % 4).astype(F32)
    member = lax.broadcasted_iota(jnp.int32, (128, 2048), 0) == owner
    s_ref[...] = jnp.where(member, 1.0, 0.0).astype(BF)
    running = jnp.zeros((128, 1), F32)
    tri = tri_ref[...]
    for c in range(8):
        at = slice(c * 256, (c + 1) * 256)
        part = s_ref[:, at]
        total = mm(part, tri) + running
        rank = jnp.sum(part.astype(F32) * total, axis=0, keepdims=True) - 1.0
        running = total[:, 255:256]
        own_ref[1:2, at] = rank.astype(jnp.int32)
    own_ref[0:1, :] = owner
    rank = own_ref[1:2, :]
    place = lax.broadcasted_iota(jnp.int32, (64, 2048), 0) == rank
    r_ref[...] = jnp.where(place, 1.0, 0.0).astype(BF)

    def grouped(value):
        return mm_nt(s_ref[...] * value, r_ref[...])

    def exact(value):
        return sum(grouped(v) for v in split3(value))

    cells = [grouped(cell_ref[c : c + 1, :].astype(F32).astype(BF)) for c in range(2)]
    fracs = [exact(frac_ref[c : c + 1, :]) for c in range(2)]
    tiles = grouped(local.astype(BF))
    msg_ref[:, 0:128] = jnp.concatenate(cells, axis=1)
    msg_ref[:, 128:256] = jnp.concatenate(fracs, axis=1)
    msg_ref[:, 256:384] = jnp.concatenate([tiles, tiles], axis=1)


def plan_floats(tile_list, float_slot, float_cell, float_frac):
    tri = np.triu(np.ones((256, 256), np.float32)).astype(jnp.bfloat16)
    return call(
        plan_kernel,
        (
            jax.ShapeDtypeStruct((128, 384), F32),
            jax.ShapeDtypeStruct((2, 2048), jnp.int32),
        ),
        [pltpu.VMEM((128, 2048), BF), pltpu.VMEM((64, 2048), BF)],
        tile_list.reshape(64, 1),
        float_slot.reshape(1, 2048),
        float_cell,
        float_frac,
        tri,
    )


def weights_of(t):
    s = 1.0 - t
    cubed = t * t * t
    return (
        s * s * s / 6.0,
        (3.0 * cubed - 6.0 * t * t + 4.0) / 6.0,
        (-3.0 * cubed + 3.0 * t * t + 3.0 * t + 1.0) / 6.0,
        cubed / 6.0,
    )


def chain(e, ws):
    zero = jnp.zeros_like(ws[0])
    out = jnp.where(e == 3.0, ws[3], zero)
    for i in (2, 1, 0):
        out = jnp.where(e == float(i), ws[i], out)
    return out


def interp_kernel(tile_ref, c_ref, msg_ref, o_ref, w_ref, r_ref):
    low = lax.broadcasted_iota(jnp.int32, (64, 128), 1) < 64

    def paired(first):
        a, b = msg_ref[0:64, first : first + 128], msg_ref[64:128, first : first + 128]
        return jnp.where(low, a, pltpu.roll(b, 64, 1)), jnp.where(low, pltpu.roll(a, 64, 1), b)

    cell0, cell1 = paired(0)
    frac0, frac1 = paired(128)
    w_ref[0] = cell0 - 1.0
    w_ref[1] = cell1 - 1.0
    for i, w in enumerate(weights_of(frac0)):
        w_ref[2 + i] = w.astype(BF).astype(F32)
    for i, w in enumerate(weights_of(frac1)):
        w_ref[6 + i] = w

    iota64 = lax.broadcasted_iota(jnp.int32, (64, 128), 0).astype(F32)
    iota128 = lax.broadcasted_iota(jnp.int32, (128, 128), 0).astype(F32)
    lowrow = lax.broadcasted_iota(jnp.int32, (1, 128), 1) < 64
    low128 = lax.broadcasted_iota(jnp.int32, (128, 128), 1) < 64

    def step(i, carry):
        ta, tb = tile_ref[i], tile_ref[i + 64]
        par = jnp.where(lowrow, (ta % 2).astype(F32), (tb % 2).astype(F32))
        rows = [w_ref[v, pl.ds(i, 1), :] for v in range(10)]
        blocks = []
        for half in range(2):
            for xp in range(2):
                base = rows[0] - 64.0 * half + 1000.0 * jnp.abs(par - xp)
                blocks.append(chain(iota64 - base, [jnp.broadcast_to(w, (64, 128)) for w in rows[2:6]]))
        down = jnp.concatenate(blocks, axis=0).astype(BF)
        across = chain(iota128 - rows[1], [jnp.broadcast_to(w, (128, 128)) for w in rows[6:10]])
        for f in range(2):
            inner = []
            for tile in (ta, tb):
                tr, xh = tile // 4, (tile % 4) // 2
                lhs = jnp.concatenate([c_ref[2 * tr, f, xh], c_ref[2 * tr + 1, f, xh]], axis=1)
                inner.append(mm(lhs, down))
            both = jnp.where(low128, inner[0], inner[1])
            r_ref[f, pl.ds(i, 1), :] = jnp.sum(both * across, axis=0, keepdims=True)
        return carry

    lax.fori_loop(0, 64, step, 0)
    u, v = r_ref[0], r_ref[1]
    o_ref[0:64, :] = jnp.where(low, u, pltpu.roll(v, 64, 1))
    o_ref[64:128, :] = jnp.where(low, pltpu.roll(u, 64, 1), v)


def interpolate(tiles, coeffs, message):
    return call(
        interp_kernel,
        jax.ShapeDtypeStruct((128, 128), F32),
        [pltpu.VMEM((10, 64, 128), F32), pltpu.VMEM((2, 64, 128), F32)],
        tiles,
        coeffs,
        message,
        specs=[
            pl.BlockSpec(memory_space=pltpu.SMEM),
            pl.BlockSpec(memory_space=pltpu.VMEM),
            pl.BlockSpec(memory_space=pltpu.VMEM),
        ],
    )


def finish_kernel(g_ref, own_ref, o_ref):
    member = lax.broadcasted_iota(jnp.int32, (128, 2048), 0) == own_ref[0:1, :]
    s = jnp.where(member, 1.0, 0.0).astype(BF)
    place = lax.broadcasted_iota(jnp.int32, (64, 2048), 0) == own_ref[1:2, :]
    t = sum(mm_tn(v, s) for v in split3(g_ref[...]))
    for c in range(2):
        o_ref[c : c + 1, :] = jnp.sum(jnp.where(place, t[c * 64 : (c + 1) * 64, :], 0.0), axis=0, keepdims=True)


def finish(speeds, own):
    return call(finish_kernel, jax.ShapeDtypeStruct((2, 2048), F32), [], speeds, own)


def shards(vorticity, tile_list, float_slot, float_cell, float_frac):
    both = ("gx", "gy")
    device = lax.axis_index(both)
    exchange = functools.partial(lax.all_to_all, split_axis=0, concat_axis=0, tiled=True)
    rows = exchange(cast_block(vorticity), "gy")
    message, own = plan_floats(tile_list, float_slot, float_cell, float_frac)
    message = exchange(message.reshape(128, 1, 384), both).reshape(128, 384)
    tiles = message[:, 256].astype(jnp.int32)
    half = exchange(rows_forward(rows.reshape(64, 64, 128)), both)
    mixed = exchange(cols_step(half, device), both)
    coeffs = exchange(rows_back(mixed), "gy")
    speeds = interpolate(tiles, coeffs, message)
    speeds = exchange(speeds.reshape(128, 1, 128), both).reshape(128, 128)
    return finish(speeds, own)


def solution(mesh):
    in_specs = (
        P("gx", "gy"),
        P(("gx", "gy"), None),
        P(("gx", "gy")),
        P(None, ("gx", "gy")),
        P(None, ("gx", "gy")),
    )
    out_specs = P(None, ("gx", "gy"))
    return jax.shard_map(shards, mesh=mesh, in_specs=in_specs, out_specs=out_specs, check_vma=False)
```

profile of v0, /device:TPU:1, one launch (start us, length us, event | category | flops | bytes accessed | tf_op | source)
XLA Modules:
  0.0 220.1 jit_solution(12562040047356038282)
XLA Ops:
  0.0 9.5 %shard_map.272 = bf16[16,4,64,128]{3,2,1,0:T(8,128)(2,1)} custom-call(f32[1024,512]{1,0:T(8,128)} %x_ref.1), custom_call_target="tpu_custom_call" | custom-call | tf_op jit(solution)/shard_map/pallas_call | solution.py:140
  9.5 23.6 %all_to_all.30 = bf16[16,4,64,128]{3,2,1,0:T(8,128)(2,1)} all-to-all(bf16[16,4,64,128]{3,2,1,0:T(8,128)(2,1)} %shard_map.272), channel_id=1, replica_groups=mesh['gx'=8,'gy'=16] {'gy'}, dimensions={0} | all-to-all | bytes 2097152 | tf_op jit(solution)/shard_map/all_to_all | solution.py:687
  33.2 11.1 %shard_map.273 = bf16[128,2,16,128]{3,2,1,0:T(8,128)(2,1)} custom-call(bf16[64,64,128]{2,1,0:T(8,128)(2,1)} %bitcast.11, f32[64,1,128]{2,1,0:T(1,128)} %constant.123.clone.twr_ref, f32[64,1,128]{2,1,0:T(1,128)} %constant.124.clone.twi_ref, bf16[128,256]{1,0:T(8,128)(2,1)} %constant.125.clone.thi_ref, bf16[128,256]{1,0:T(8,128)(2,1)} %constant.126.clone.tlo_ref, ...), custom_call_target="tpu_custom_call" | custom-call | tf_op jit(solution)/shard_map/pallas_call | solution.py:122
  44.3 8.7 %all-to-all-start.2 = ((bf16[128,2,16,128]{3,2,1,0:T(8,128)(2,1)}), bf16[128,2,16,128]{3,2,1,0:T(8,128)(2,1)S(1)}, u32[]{:S(2)}, u32[]{:S(2)}) async-start(bf16[128,2,16,128]{3,2,1,0:T(8,128)(2,1)} %shard_map.273), calls=%async_computation.2 | async-start | bytes 2097152 | tf_op jit(solution)/shard_map/all_to_all | solution.py:691
  53.0 0.7 fusion.2
  53.7 18.0 %all-to-all-done.2.x_ref = bf16[128,2,16,128]{3,2,1,0:T(8,128)(2,1)S(1)} async-done(((bf16[128,2,16,128]{3,2,1,0:T(8,128)(2,1)}), bf16[128,2,16,128]{3,2,1,0:T(8,128)(2,1)S(1)}, u32[]{:S(2)}, u32[]{:S(2)}) %all-to-all-start.2) | async-done | bytes 1048608 | tf_op jit(solution)/shard_map/all_to_all | solution.py:691
  71.8 0.0 copy-start.2
  71.8 1.0 copy-done.2
  72.8 15.9 %shard_map.274 = bf16[128,2,2,16,128]{4,3,2,1,0:T(8,128)(2,1)} custom-call(bf16[128,2,16,128]{3,2,1,0:T(8,128)(2,1)} %copy-done.2, f32[128,1,128]{2,1,0:T(1,128)} %constant.128.clone.twr_ref, f32[128,1,128]{2,1,0:T(1,128)} %constant.129.clone.twi_ref, f32[128,128]{1,0:T(8,128)} %constant.130.clone.tw2r_ref, f32[128,128]{1,0:T(8,128)} %constant.131.clone.tw2i_ref, ...), custom_call_target="tpu_custom_call" | custom-call | tf_op jit(solution)/shard_map/pallas_call | solution.py:122
  88.7 0.0 copy-start.4
  88.7 4.8 %all-to-all-start.3 = ((bf16[128,2,2,16,128]{4,3,2,1,0:T(8,128)(2,1)}), bf16[128,2,2,16,128]{4,3,2,1,0:T(8,128)(2,1)S(1)}, u32[]{:S(2)}, u32[]{:S(2)}) async-start(bf16[128,2,2,16,128]{4,3,2,1,0:T(8,128)(2,1)} %shard_map.274), calls=%async_computation.3 | async-start | bytes 4194304 | tf_op jit(solution)/shard_map/all_to_all | solution.py:692
  93.5 0.0 copy-done.4
  93.5 0.7 copy.32.list_ref
  94.2 4.1 %shard_map.271 = (f32[128,384]{1,0:T(8,128)}, s32[2,2048]{1,0:T(2,128)}) custom-call(s32[64,1]{1,0:T(8,128)} %copy.32.list_ref, s32[1,2048]{1,0:T(1,128)} %bitcast.17, s32[2,2048]{1,0:T(2,128)} %cell_ref.1, f32[2,2048]{1,0:T(2,128)} %frac_ref.1, bf16[256,256]{1,0:T(8,128)(2,1)} %constant.122.clone.tri_ref), custom_call_target="tpu_custom_call" | custom-call | tf_op jit(solution)/shard_map/pallas_call | solution.py:122
  98.3 1.8 copy.33
  100.1 23.3 %all-to-all-done.3.x_ref = bf16[128,2,2,16,128]{4,3,2,1,0:T(8,128)(2,1)S(1)} async-done(((bf16[128,2,2,16,128]{4,3,2,1,0:T(8,128)(2,1)}), bf16[128,2,2,16,128]{4,3,2,1,0:T(8,128)(2,1)S(1)}, u32[]{:S(2)}, u32[]{:S(2)}) %all-to-all-start.3) | async-done | bytes 2097184 | tf_op jit(solution)/shard_map/all_to_all | solution.py:692
  123.4 0.0 copy-start.1
  123.4 4.5 %all-to-all-start = ((f32[128,1,384]{2,1,0:T(1,128)}), f32[128,1,384]{2,1,0:T(1,128)S(1)}, u32[]{:S(2)}, u32[]{:S(2)}) async-start(f32[128,1,384]{2,1,0:T(1,128)} %copy.33), calls=%async_computation | async-start | bytes 393216 | tf_op jit(solution)/shard_map/all_to_all | solution.py:689
  127.9 0.0 copy-done.1
  127.9 15.2 %shard_map.275 = bf16[16,2,2,128,128]{4,3,2,1,0:T(8,128)(2,1)} custom-call(bf16[128,2,2,16,128]{4,3,2,1,0:T(8,128)(2,1)} %copy-done.1, bf16[256,256]{1,0:T(8,128)(2,1)} %constant.140.clone.t_ref, f32[128,128]{1,0:T(8,128)} %constant.141.clone.t0r_ref, f32[128,128]{1,0:T(8,128)} %constant.142.clone.t0i_ref, f32[128,128]{1,0:T(8,128)} %constant.143.clone.omr_ref, ...), custom_call_target="tpu_custom_call" | custom-call | tf_op jit(solution)/shard_map/pallas_call | solution.py:122
  143.1 0.0 all-to-all-done
  143.1 6.8 %all-to-all-start.4 = ((bf16[16,2,2,128,128]{4,3,2,1,0:T(8,128)(2,1)}), bf16[16,2,2,128,128]{4,3,2,1,0:T(8,128)(2,1)S(1)}, u32[]{:S(2)}, u32[]{:S(2)}) async-start(bf16[16,2,2,128,128]{4,3,2,1,0:T(8,128)(2,1)} %shard_map.275), calls=%async_computation.4 | async-start | bytes 4194304 | tf_op jit(solution)/shard_map/all_to_all | solution.py:693
  150.0 0.0 copy-start.3
  150.0 0.6 fusion.tile_ref
  150.6 28.5 %all-to-all-done.4.c_ref = bf16[16,2,2,128,128]{4,3,2,1,0:T(8,128)(2,1)S(1)} async-done(((bf16[16,2,2,128,128]{4,3,2,1,0:T(8,128)(2,1)}), bf16[16,2,2,128,128]{4,3,2,1,0:T(8,128)(2,1)S(1)}, u32[]{:S(2)}, u32[]{:S(2)}) %all-to-all-start.4) | async-done | bytes 2097184 | tf_op jit(solution)/shard_map/all_to_all | solution.py:693
  179.1 0.0 copy-done.3
  179.1 0.0 copy-start
  179.1 1.3 copy-done
  180.5 19.0 %shard_map.276 = f32[128,128]{1,0:T(8,128)} custom-call(s32[128]{0:T(128)} %fusion.tile_ref, bf16[16,2,2,128,128]{4,3,2,1,0:T(8,128)(2,1)} %copy-done, f32[128,384]{1,0:T(8,128)} %bitcast.13), custom_call_target="tpu_custom_call" | custom-call | tf_op jit(solution)/shard_map/pallas_call | solution.py:122
  199.4 18.6 %all_to_all.31 = f32[128,1,128]{2,1,0:T(1,128)} all-to-all(f32[128,1,128]{2,1,0:T(1,128)} %bitcast.14), channel_id=1, replica_groups=mesh['gx'=8,'gy'=16] {'gx','gy'}, dimensions={0} | all-to-all | bytes 131072 | tf_op jit(solution)/shard_map/all_to_all | solution.py:695
  218.0 2.1 shard_map.277
  (4 shorter events, 0.0 us)
Async XLA Ops:
  44.3 27.5 %all-to-all-start.2 = ((bf16[128,2,16,128]{3,2,1,0:T(8,128)(2,1)}), bf16[128,2,16,128]{3,2,1,0:T(8,128)(2,1)S(1)}, u32[]{:S(2)}, u32[]{:S(2)}) async-start(bf16[128,2,16,128]{3,2,1,0:T(8,128)(2,1)} %shard_map.273), calls=%async_computation.2 | async-start | bytes 2097152 | tf_op jit(solution)/shard_map/all_to_all | solution.py:691
  71.8 1.0 copy-start.2
  88.7 4.8 %copy-start.4 = (s32[1,64]{1,0:T(1,128)S(1)}, s32[1,64]{1,0:T(1,128)}, u32[]{:S(2)}) copy-start(s32[1,64]{1,0:T(1,128)} %param.30) | copy-start | bytes 772
  88.7 34.7 %all-to-all-start.3 = ((bf16[128,2,2,16,128]{4,3,2,1,0:T(8,128)(2,1)}), bf16[128,2,2,16,128]{4,3,2,1,0:T(8,128)(2,1)S(1)}, u32[]{:S(2)}, u32[]{:S(2)}) async-start(bf16[128,2,2,16,128]{4,3,2,1,0:T(8,128)(2,1)} %shard_map.274), calls=%async_computation.3 | async-start | bytes 4194304 | tf_op jit(solution)/shard_map/all_to_all | solution.py:692
  123.4 4.5 %copy-start.1 = (bf16[128,2,2,16,128]{4,3,2,1,0:T(8,128)(2,1)}, bf16[128,2,2,16,128]{4,3,2,1,0:T(8,128)(2,1)S(1)}, u32[]{:S(2)}) copy-start(bf16[128,2,2,16,128]{4,3,2,1,0:T(8,128)(2,1)S(1)} %all-to-all-done.3.x_ref) | copy-start | bytes 6291460
  123.4 19.7 %all-to-all-start = ((f32[128,1,384]{2,1,0:T(1,128)}), f32[128,1,384]{2,1,0:T(1,128)S(1)}, u32[]{:S(2)}, u32[]{:S(2)}) async-start(f32[128,1,384]{2,1,0:T(1,128)} %copy.33), calls=%async_computation | async-start | bytes 393216 | tf_op jit(solution)/shard_map/all_to_all | solution.py:689
  143.1 36.0 %all-to-all-start.4 = ((bf16[16,2,2,128,128]{4,3,2,1,0:T(8,128)(2,1)}), bf16[16,2,2,128,128]{4,3,2,1,0:T(8,128)(2,1)S(1)}, u32[]{:S(2)}, u32[]{:S(2)}) async-start(bf16[16,2,2,128,128]{4,3,2,1,0:T(8,128)(2,1)} %shard_map.275), calls=%async_computation.4 | async-start | bytes 4194304 | tf_op jit(solution)/shard_map/all_to_all | solution.py:693
  150.0 29.2 %copy-start.3 = (f32[128,1,384]{2,0,1:T(8,128)}, f32[128,1,384]{2,0,1:T(8,128)S(1)}, u32[]{:S(2)}) copy-start(f32[128,1,384]{2,0,1:T(8,128)S(1)} %copy.37) | copy-start | bytes 589828
  179.1 1.3 copy-start
where the time goes:
time: 221 us; the launch traced here: 220 us
  Pallas kernels  76.9 us (35%)
  waiting for transfers between devices  69.9 us (32%)
  blocking collectives  42.2 us (19%)
  starting transfers between devices  24.8 us (11%)
  local copies, waits for them, and re-layouts  4.83 us (2%)
    pallas_call x6, Pallas kernels, call(): return pl.pallas_call(kernel, **params)(*args)  67.3 us
    all_to_all x1, waiting for transfers between devices, shards(): coeffs = exchange(rows_back(mixed), 'gy')  28.5 us
    all_to_all x1, blocking collectives, shards(): rows = exchange(cast_block(vorticity), 'gy')  23.6 us
    all_to_all x1, waiting for transfers between devices, shards(): mixed = exchange(cols_step(half, device), both)  23.3 us
    all_to_all x1, blocking collectives, shards(): speeds = exchange(speeds.reshape(128, 1, 128), both).reshape(128, 128)  18.6 us
    all_to_all x1, waiting for transfers between devices, shards(): half = exchange(rows_forward(rows.reshape(64, 64, 128)), both)  18 us
    pallas_call x1, Pallas kernels, cast_block(): pl.pallas_call(cast_kernel, grid=(16,), in_specs=[pl.BlockSpec((64, 512),...  9.55 us
    all_to_all x1, starting transfers between devices, shards(): half = exchange(rows_forward(rows.reshape(64, 64, 128)), both)  8.67 us
  transfers between devices with their start and end apart: 4, of which 3 were waited for; matrix products, arithmetic and copies ran while one was open for 2% of the time, Pallas kernels for 9%

commit v1 on v0

--- a/solution.py
+++ b/solution.py
@@ -13,7 +13,7 @@
 KAPPA = math.pi / N
 BF = jnp.bfloat16
 F32 = jnp.float32
-VMEM = 60 * 1024 * 1024
+VMEM = 30 * 1024 * 1024
 
 
 def _mul_const(v, c, s):
@@ -129,24 +129,25 @@
         error = jnp.where(rows, x.astype(BF).astype(F32) - x, 0.0)
         return x - pltpu.roll(error, shift, 1)
 
-    for q in range(4):
-        x = x_ref[:, q * 128 : (q + 1) * 128].reshape(8, 8, 128)
-        x = handed(x, s % 2 == 0, 1)
-        x = handed(x, s % 4 == 1, 2)
-        o_ref[0, q] = x.reshape(64, 128).astype(BF)
+    for d in range(4):
+        for q in range(4):
+            x = x_ref[d * 64 : (d + 1) * 64, q * 128 : (q + 1) * 128].reshape(8, 8, 128)
+            x = handed(x, s % 2 == 0, 1)
+            x = handed(x, s % 4 == 1, 2)
+            o_ref[d, q] = x.reshape(64, 128).astype(BF)
 
 
 def cast_block(vorticity):
     return pl.pallas_call(
         cast_kernel,
-        grid=(16,),
-        in_specs=[pl.BlockSpec((64, 512), lambda i: (i, 0))],
-        out_specs=pl.BlockSpec((1, 4, 64, 128), lambda i: (i, 0, 0, 0)),
+        grid=(4,),
+        in_specs=[pl.BlockSpec((256, 512), lambda i: (i, 0))],
+        out_specs=pl.BlockSpec((4, 4, 64, 128), lambda i: (i, 0, 0, 0)),
         out_shape=jax.ShapeDtypeStruct((16, 4, 64, 128), BF),
     )(vorticity)
 
 
-def rows_kernel(x_ref, twr_ref, twi_ref, thi_ref, tlo_ref, alt_ref, o_ref, a_ref, yhi_ref, ylo_ref):
+def rows_kernel(x_ref, m_ref, twr_ref, twi_ref, thi_ref, tlo_ref, alt_ref, o_ref, a_ref, yhi_ref, ylo_ref):
     def first(t, carry):
         rows = pl.ds(pl.multiple_of(t * 16, 16), 16)
         for j in range(8):
@@ -193,18 +194,19 @@
         zb = z.astype(BF)
         for g in range(4):
             for c in range(2):
-                o_ref[4 * kap + g, c] = zb[c * 64 + 16 * g : c * 64 + 16 * g + 16, :]
-        return carry
-
-    lax.fori_loop(0, 32, third, 0)
+                o_ref[4 * kap + g, 16 * c : 16 * c + 16, :] = zb[c * 64 + 16 * g : c * 64 + 16 * g + 16, :]
+            o_ref[4 * kap + g, 32:40, :] = m_ref[4 * kap + g]
+        return carry
+
+    lax.fori_loop(0, 32, third, 0, unroll=4)
 
     nyq = mm_nt(alt_ref[...], yhi_ref[0:2].reshape(128, 256)) + mm_nt(
         alt_ref[...], ylo_ref[0:2].reshape(128, 256)
     )
     lane = lax.broadcasted_iota(jnp.int32, (16, 128), 1)
     sub = lax.broadcasted_iota(jnp.int32, (16, 128), 0)
-    old = o_ref[0, 1].astype(F32)
-    o_ref[0, 1] = jnp.where((lane < 64) & (sub == 0), nyq, old).astype(BF)
+    old = o_ref[0, 16:32, :].astype(F32)
+    o_ref[0, 16:32, :] = jnp.where((lane < 64) & (sub == 0), nyq, old).astype(BF)
 
 
 @functools.cache
@@ -226,16 +228,17 @@
     )
 
 
-def rows_forward(x):
+def rows_forward(x, message):
     return call(
         rows_kernel,
-        jax.ShapeDtypeStruct((128, 2, 16, 128), BF),
+        jax.ShapeDtypeStruct((128, 40, 128), BF),
         [
             pltpu.VMEM((5, 8, 2, 64, 128), F32),
             pltpu.VMEM((64, 64, 256), BF),
             pltpu.VMEM((64, 64, 256), BF),
         ],
         x,
+        message,
         *rows_tables(),
     )
 
@@ -262,7 +265,8 @@
 ):
     def widen(t, carry):
         for u in range(8):
-            x32_ref[8 * t + u] = x_ref[8 * t + u].astype(F32)
+            for c in range(2):
+                x32_ref[8 * t + u, c] = x_ref[8 * t + u, 16 * c : 16 * c + 16, :].astype(F32)
         return carry
 
     lax.fori_loop(0, 16, widen, 0)
@@ -456,7 +460,7 @@
         s_ref[kap] = mm(table, jnp.concatenate(cols, axis=1))
         return carry
 
-    lax.fori_loop(0, 32, first, 0)
+    lax.fori_loop(0, 32, first, 0, unroll=4)
 
     row = x_ref[0, 0, 1].astype(F32)[0:1, :]
     lane = lax.broadcasted_iota(jnp.int32, (128, 128), 1)
@@ -530,7 +534,7 @@
     return hi, mid, (rest - mid.astype(F32)).astype(BF)
 
 
-def plan_kernel(list_ref, slot_ref, cell_ref, frac_ref, tri_ref, msg_ref, own_ref, s_ref, r_ref):
+def plan_kernel(list_ref, slot_ref, cell_ref, frac_ref, tri_ref, msg_ref, own_ref, s_ref, r_ref, v_ref):
     slot = slot_ref[...]
     pick = lax.broadcasted_iota(jnp.int32, (64, 2048), 0) == slot
     tile = jnp.sum(jnp.where(pick, list_ref[...], 0), axis=0, keepdims=True)
@@ -550,21 +554,24 @@
         own_ref[1:2, at] = rank.astype(jnp.int32)
     own_ref[0:1, :] = owner
     rank = own_ref[1:2, :]
-    place = lax.broadcasted_iota(jnp.int32, (64, 2048), 0) == rank
+    place = lax.broadcasted_iota(jnp.int32, (128, 2048), 0) == rank
     r_ref[...] = jnp.where(place, 1.0, 0.0).astype(BF)
-
-    def grouped(value):
-        return mm_nt(s_ref[...] * value, r_ref[...])
-
-    def exact(value):
-        return sum(grouped(v) for v in split3(value))
-
-    cells = [grouped(cell_ref[c : c + 1, :].astype(F32).astype(BF)) for c in range(2)]
-    fracs = [exact(frac_ref[c : c + 1, :]) for c in range(2)]
-    tiles = grouped(local.astype(BF))
-    msg_ref[:, 0:128] = jnp.concatenate(cells, axis=1)
-    msg_ref[:, 128:256] = jnp.concatenate(fracs, axis=1)
-    msg_ref[:, 256:384] = jnp.concatenate([tiles, tiles], axis=1)
+    hi0, lo0 = split2(frac_ref[0:1, :])
+    hi1, lo1 = split2(frac_ref[1:2, :])
+    parts = [cell_ref[0:1, :], cell_ref[1:2, :], local, hi0, lo0, hi1, lo1]
+    sub = lax.broadcasted_iota(jnp.int32, (16, 2048), 0)
+    values = jnp.zeros((16, 2048), F32)
+    for v, part in enumerate(parts):
+        values = jnp.where(sub % 8 == v, part.astype(F32), values)
+    pair = owner - sub // 8
+
+    def spread(t, carry):
+        v_ref[pl.ds(pl.multiple_of(16 * t, 16), 16), :] = jnp.where(pair == 2 * t, values, 0.0).astype(BF)
+        return carry
+
+    lax.fori_loop(0, 64, spread, 0, unroll=2)
+    out = mm_nt(v_ref[...], r_ref[...]).astype(BF)
+    msg_ref[...] = out.reshape(128, 8, 128)
 
 
 def plan_floats(tile_list, float_slot, float_cell, float_frac):
@@ -572,10 +579,10 @@
     return call(
         plan_kernel,
         (
-            jax.ShapeDtypeStruct((128, 384), F32),
+            jax.ShapeDtypeStruct((128, 8, 128), BF),
             jax.ShapeDtypeStruct((2, 2048), jnp.int32),
         ),
-        [pltpu.VMEM((128, 2048), BF), pltpu.VMEM((64, 2048), BF)],
+        [pltpu.VMEM((128, 2048), BF), pltpu.VMEM((128, 2048), BF), pltpu.VMEM((1024, 2048), BF)],
         tile_list.reshape(64, 1),
         float_slot.reshape(1, 2048),
         float_cell,
@@ -603,20 +610,21 @@
     return out
 
 
-def interp_kernel(tile_ref, c_ref, msg_ref, o_ref, w_ref, r_ref):
+def interp_kernel(tile_ref, c_ref, msg_ref, o_ref, m_ref, w_ref, r_ref):
     low = lax.broadcasted_iota(jnp.int32, (64, 128), 1) < 64
-
-    def paired(first):
-        a, b = msg_ref[0:64, first : first + 128], msg_ref[64:128, first : first + 128]
-        return jnp.where(low, a, pltpu.roll(b, 64, 1)), jnp.where(low, pltpu.roll(a, 64, 1), b)
-
-    cell0, cell1 = paired(0)
-    frac0, frac1 = paired(128)
-    w_ref[0] = cell0 - 1.0
-    w_ref[1] = cell1 - 1.0
-    for i, w in enumerate(weights_of(frac0)):
+    low8 = lax.broadcasted_iota(jnp.int32, (8, 128), 1) < 64
+    for i in range(64):
+        other = pltpu.roll(msg_ref[i + 64].astype(F32), 64, 1)
+        m_ref[8 * i : 8 * i + 8, :] = jnp.where(low8, msg_ref[i].astype(F32), other)
+
+    def row(v):
+        return m_ref[pl.ds(v, 64, stride=8), :]
+
+    w_ref[0] = row(0) - 1.0
+    w_ref[1] = row(1) - 1.0
+    for i, w in enumerate(weights_of(row(3) + row(4))):
         w_ref[2 + i] = w.astype(BF).astype(F32)
-    for i, w in enumerate(weights_of(frac1)):
+    for i, w in enumerate(weights_of(row(5) + row(6))):
         w_ref[6 + i] = w
 
     iota64 = lax.broadcasted_iota(jnp.int32, (64, 128), 0).astype(F32)
@@ -645,7 +653,7 @@
             r_ref[f, pl.ds(i, 1), :] = jnp.sum(both * across, axis=0, keepdims=True)
         return carry
 
-    lax.fori_loop(0, 64, step, 0)
+    lax.fori_loop(0, 64, step, 0, unroll=4)
     u, v = r_ref[0], r_ref[1]
     o_ref[0:64, :] = jnp.where(low, u, pltpu.roll(v, 64, 1))
     o_ref[64:128, :] = jnp.where(low, pltpu.roll(u, 64, 1), v)
@@ -655,7 +663,11 @@
     return call(
         interp_kernel,
         jax.ShapeDtypeStruct((128, 128), F32),
-        [pltpu.VMEM((10, 64, 128), F32), pltpu.VMEM((2, 64, 128), F32)],
+        [
+            pltpu.VMEM((512, 128), F32),
+            pltpu.VMEM((10, 64, 128), F32),
+            pltpu.VMEM((2, 64, 128), F32),
+        ],
         tiles,
         coeffs,
         message,
@@ -686,9 +698,9 @@
     exchange = functools.partial(lax.all_to_all, split_axis=0, concat_axis=0, tiled=True)
     rows = exchange(cast_block(vorticity), "gy")
     message, own = plan_floats(tile_list, float_slot, float_cell, float_frac)
-    message = exchange(message.reshape(128, 1, 384), both).reshape(128, 384)
-    tiles = message[:, 256].astype(jnp.int32)
-    half = exchange(rows_forward(rows.reshape(64, 64, 128)), both)
+    half = exchange(rows_forward(rows.reshape(64, 64, 128), message), both)
+    message = half[:, 32:40, :]
+    tiles = message[:, 2, 0].astype(jnp.int32)
     mixed = exchange(cols_step(half, device), both)
     coeffs = exchange(rows_back(mixed), "gy")
     speeds = interpolate(tiles, coeffs, message)

time: 221 us -> 181 us (0.82)
  Pallas kernels: 76.9 us -> 46.3 us
  waiting for transfers between devices: 69.9 us -> 56.4 us
  blocking collectives: 42.2 us -> 52.6 us
  starting transfers between devices: 24.8 us -> 20.5 us
  local copies, waits for them, and re-layouts: 4.83 us -> 1.93 us
    pallas_call x6, Pallas kernels: 67.3 us -> 42.2 us  [call(): return pl.pallas_call(kernel, **params)(*args)]
    all_to_all x1, blocking collectives: 23.6 us -> 34.3 us  [shards(): mixed = exchange(cols_step(half, device), both)]
    all_to_all x3 -> x2, waiting for transfers between devices: 41.3 us -> 33.4 us  [the longest x1 21.1 us: shards(): half = exchange(rows_forward(rows.reshape(64, 64, 128), message), both)]
    all_to_all x1, waiting for transfers between devices: 28.5 us -> 23 us  [shards(): coeffs = exchange(rows_back(mixed), 'gy')]
    pallas_call x1, Pallas kernels: 9.55 us -> 4.1 us  [cast_block(): pl.pallas_call(cast_kernel, grid=(4,), in_specs=[pl.BlockSpec((256, 512),...]
    all_to_all x1, starting transfers between devices: 6.8 us -> 3.72 us  [shards(): coeffs = exchange(rows_back(mixed), 'gy')]
    all_to_all x3 -> x2, starting transfers between devices: 18 us -> 16.8 us  [the longest x1 9.24 us: shards(): half = exchange(rows_forward(rows.reshape(64, 64, 128), message), both)]
  transfers between devices with their start and end apart: 4 -> 3, of which waited for: 3 -> 3; matrix products, arithmetic and copies ran while one was open for 2% -> 2% of each run, Pallas kernels for 9% -> 2%
where the time goes in v1:
time: 181 us
  waiting for transfers between devices  56.4 us (31%)
  blocking collectives  52.6 us (29%)
  Pallas kernels  46.3 us (26%)
  starting transfers between devices  20.5 us (11%)
  other arithmetic  2.5 us (1%)
  local copies, waits for them, and re-layouts  1.93 us (1%)
    pallas_call x6, Pallas kernels, call(): return pl.pallas_call(kernel, **params)(*args)  42.2 us
    all_to_all x1, blocking collectives, shards(): mixed = exchange(cols_step(half, device), both)  34.3 us
    all_to_all x1, waiting for transfers between devices, shards(): coeffs = exchange(rows_back(mixed), 'gy')  23 us
    all_to_all x1, waiting for transfers between devices, shards(): half = exchange(rows_forward(rows.reshape(64, 64, 128), message), both)  21.1 us
    all_to_all x1, blocking collectives, shards(): speeds = exchange(speeds.reshape(128, 1, 128), both).reshape(128, 128)  18.4 us
    all_to_all x1, waiting for transfers between devices, shards(): rows = exchange(cast_block(vorticity), 'gy')  12.3 us
    all_to_all x1, starting transfers between devices, shards(): half = exchange(rows_forward(rows.reshape(64, 64, 128), message), both)  9.24 us
    all_to_all x1, starting transfers between devices, shards(): rows = exchange(cast_block(vorticity), 'gy')  7.57 us
  transfers between devices with their start and end apart: 3, of which 3 were waited for; matrix products, arithmetic and copies ran while one was open for 2% of the time, Pallas kernels for 2%

profile of v1, /device:TPU:1, one launch (start us, length us, event | category | flops | bytes accessed | tf_op | source)
XLA Modules:
  0.0 180.8 jit_solution(10149545601992580330)
XLA Ops:
  0.0 0.0 copy-start.22
  0.0 0.0 copy-start.23
  0.0 0.0 copy-start.26
  0.1 4.1 %shard_map.271 = bf16[16,4,64,128]{3,2,1,0:T(8,128)(2,1)} custom-call(f32[1024,512]{1,0:T(8,128)} %x_ref.1), custom_call_target="tpu_custom_call" | custom-call | tf_op jit(solution)/shard_map/pallas_call | solution.py:141
  4.2 7.6 %all-to-all-start = ((bf16[16,4,64,128]{3,2,1,0:T(8,128)(2,1)}), bf16[16,4,64,128]{3,2,1,0:T(8,128)(2,1)S(1)}, u32[]{:S(2)}, u32[]{:S(2)}) async-start(bf16[16,4,64,128]{3,2,1,0:T(8,128)(2,1)} %shard_map.271), calls=%async_computation | async-start | bytes 2097152 | tf_op jit(solution)/shard_map/all_to_all | solution.py:699
  11.8 0.1 copy.32.list_ref
  11.9 3.2 %shard_map.272 = (bf16[128,8,128]{2,1,0:T(8,128)(2,1)S(1)}, s32[2,2048]{1,0:T(2,128)S(1)}) custom-call(s32[64,1]{1,0:T(8,128)S(1)} %copy.32.list_ref, s32[1,2048]{1,0:T(1,128)S(1)} %bitcast.10, s32[2,2048]{1,0:T(2,128)S(1)} %copy-done.24, f32[2,2048]{1,0:T(2,128)S(1)} %copy-done.25, bf16[256,256]{1,0:T(8,128)(2,1)S(1)} %copy-done.6), custom_call_target="tpu_custom_call" | custom-call | tf_op jit(solution)/shard_map/pallas_call | solution.py:122
  15.1 12.3 %all-to-all-done = bf16[16,4,64,128]{3,2,1,0:T(8,128)(2,1)S(1)} async-done(((bf16[16,4,64,128]{3,2,1,0:T(8,128)(2,1)}), bf16[16,4,64,128]{3,2,1,0:T(8,128)(2,1)S(1)}, u32[]{:S(2)}, u32[]{:S(2)}) %all-to-all-start) | async-done | bytes 1048608 | tf_op jit(solution)/shard_map/all_to_all | solution.py:699
  27.4 0.0 copy-done.22
  27.5 0.0 copy-start.2
  27.5 0.0 copy-start.3
  27.5 0.0 copy-start.4
  27.5 0.0 copy-start.5
  27.5 0.0 copy-start.12
  27.5 0.0 copy-start.13
  27.5 0.0 copy-start.14
  27.6 0.0 copy-start.15
  27.6 0.0 copy-start.16
  27.6 0.0 copy-start.17
  27.6 6.0 %shard_map.273 = bf16[128,40,128]{2,1,0:T(8,128)(2,1)} custom-call(bf16[64,64,128]{2,1,0:T(8,128)(2,1)S(1)} %bitcast.7, bf16[128,8,128]{2,1,0:T(8,128)(2,1)S(1)} %get-tuple-element.7.m_ref, f32[64,1,128]{2,1,0:T(1,128)S(1)} %copy-done.23, f32[64,1,128]{2,1,0:T(1,128)S(1)} %copy-done.22, bf16[128,256]{1,0:T(8,128)(2,1)S(1)} %copy-done.21, ...), custom_call_target="tpu_custom_call" | custom-call | tf_op jit(solution)/shard_map/pallas_call | solution.py:122
  33.6 9.2 %all-to-all-start.1 = ((bf16[128,40,128]{2,1,0:T(8,128)(2,1)}), bf16[128,40,128]{2,1,0:T(8,128)(2,1)S(1)}, u32[]{:S(2)}, u32[]{:S(2)}) async-start(bf16[128,40,128]{2,1,0:T(8,128)(2,1)} %shard_map.273), calls=%async_computation.1 | async-start | bytes 2621440 | tf_op jit(solution)/shard_map/all_to_all | solution.py:701
  42.9 0.1 fusion.2
  43.0 21.1 %all-to-all-done.1.x_ref = bf16[128,40,128]{2,1,0:T(8,128)(2,1)S(1)} async-done(((bf16[128,40,128]{2,1,0:T(8,128)(2,1)}), bf16[128,40,128]{2,1,0:T(8,128)(2,1)S(1)}, u32[]{:S(2)}, u32[]{:S(2)}) %all-to-all-start.1) | async-done | bytes 1310752 | tf_op jit(solution)/shard_map/all_to_all | solution.py:701
  64.2 0.0 copy-done.4
  64.2 0.0 copy-done.5
  64.2 0.0 copy-done.12
  64.2 0.0 copy-done.13
  64.2 0.0 copy-done.14
  64.2 0.0 copy-done.15
  64.2 0.0 copy-done.16
  64.2 0.0 copy-done.17
  64.3 13.4 %shard_map.274 = bf16[128,2,2,16,128]{4,3,2,1,0:T(8,128)(2,1)S(1)} custom-call(bf16[128,40,128]{2,1,0:T(8,128)(2,1)S(1)} %all-to-all-done.1.x_ref, f32[128,1,128]{2,1,0:T(1,128)S(1)} %copy-done.19, f32[128,1,128]{2,1,0:T(1,128)S(1)} %copy-done.18, f32[128,128]{1,0:T(8,128)S(1)} %copy-done.17, f32[128,128]{1,0:T(8,128)S(1)} %copy-done.16, ...), custom_call_target="tpu_custom_call" | custom-call | tf_op jit(solution)/shard_map/pallas_call | solution.py:122
  77.6 0.0 copy-start.1
  77.6 0.0 copy-start.7
  77.7 0.0 copy-start.8
  77.7 0.0 copy-start.9
  77.7 0.0 copy-start.10
  77.7 0.0 copy-start.11
  77.7 34.3 %all_to_all.25.x_ref = bf16[128,2,2,16,128]{4,3,2,1,0:T(8,128)(2,1)S(1)} all-to-all(bf16[128,2,2,16,128]{4,3,2,1,0:T(8,128)(2,1)S(1)} %shard_map.274), channel_id=1, replica_groups=mesh['gx'=8,'gy'=16] {'gx','gy'}, dimensions={0} | all-to-all | bytes 4194304 | tf_op jit(solution)/shard_map/all_to_all | solution.py:704
  112.0 9.8 %shard_map.275 = bf16[16,2,2,128,128]{4,3,2,1,0:T(8,128)(2,1)} custom-call(bf16[128,2,2,16,128]{4,3,2,1,0:T(8,128)(2,1)S(1)} %all_to_all.25.x_ref, bf16[256,256]{1,0:T(8,128)(2,1)S(1)} %copy-done.1, f32[128,128]{1,0:T(8,128)S(1)} %copy-done.11, f32[128,128]{1,0:T(8,128)S(1)} %copy-done.10, f32[128,128]{1,0:T(8,128)S(1)} %copy-done.9, ...), custom_call_target="tpu_custom_call" | custom-call | tf_op jit(solution)/shard_map/pallas_call | solution.py:122
  121.9 3.7 %all-to-all-start.3 = ((bf16[16,2,2,128,128]{4,3,2,1,0:T(8,128)(2,1)}), bf16[16,2,2,128,128]{4,3,2,1,0:T(8,128)(2,1)S(1)}, u32[]{:S(2)}, u32[]{:S(2)}) async-start(bf16[16,2,2,128,128]{4,3,2,1,0:T(8,128)(2,1)} %shard_map.275), calls=%async_computation.3 | async-start | bytes 4194304 | tf_op jit(solution)/shard_map/all_to_all | solution.py:705
  125.6 0.7 slice.10.msg_ref
  126.3 2.4 %fusion.tile_ref = s32[128]{0:T(128)S(1)} fusion(bf16[128,40,128]{2,1,0:T(8,128)(2,1)S(1)} %all-to-all-done.1.x_ref), kind=kLoop, calls=%fused_computation.1 | loop fusion | flops 128 | bytes 768 | tf_op jit(solution)/shard_map/convert_element_type | solution.py:703
  128.7 23.0 %all-to-all-done.3.c_ref = bf16[16,2,2,128,128]{4,3,2,1,0:T(8,128)(2,1)S(1)} async-done(((bf16[16,2,2,128,128]{4,3,2,1,0:T(8,128)(2,1)}), bf16[16,2,2,128,128]{4,3,2,1,0:T(8,128)(2,1)S(1)}, u32[]{:S(2)}, u32[]{:S(2)}) %all-to-all-start.3) | async-done | bytes 2097184 | tf_op jit(solution)/shard_map/all_to_all | solution.py:705
  151.7 0.9 copy-done
  152.6 8.5 %shard_map.276 = f32[128,128]{1,0:T(8,128)S(1)} custom-call(s32[128]{0:T(128)S(1)} %fusion.tile_ref, bf16[16,2,2,128,128]{4,3,2,1,0:T(8,128)(2,1)S(1)} %all-to-all-done.3.c_ref, bf16[128,8,128]{2,1,0:T(8,128)(2,1)S(1)} %copy-done), custom_call_target="tpu_custom_call" | custom-call | tf_op jit(solution)/shard_map/pallas_call | solution.py:122
  161.2 18.4 %all_to_all.26 = f32[128,1,128]{2,1,0:T(1,128)S(1)} all-to-all(f32[128,1,128]{2,1,0:T(1,128)S(1)} %bitcast.9), channel_id=1, replica_groups=mesh['gx'=8,'gy'=16] {'gx','gy'}, dimensions={0} | all-to-all | bytes 131072 | tf_op jit(solution)/shard_map/all_to_all | solution.py:707
  179.5 1.2 shard_map.277
  (32 shorter events, 0.1 us)
Async XLA Ops:
  0.0 11.9 %copy-start.6 = (bf16[256,256]{1,0:T(8,128)(2,1)S(1)}, bf16[256,256]{1,0:T(8,128)(2,1)}, u32[]{:S(2)}) copy-start(bf16[256,256]{1,0:T(8,128)(2,1)} %constant.122.clone.tri_ref) | copy-start | bytes 393220
  0.0 27.4 %copy-start.20 = (bf16[128,256]{1,0:T(8,128)(2,1)S(1)}, bf16[128,256]{1,0:T(8,128)(2,1)}, u32[]{:S(2)}) copy-start(bf16[128,256]{1,0:T(8,128)(2,1)} %constant.126.clone.tlo_ref) | copy-start | bytes 196612
  0.0 27.4 %copy-start.21 = (bf16[128,256]{1,0:T(8,128)(2,1)S(1)}, bf16[128,256]{1,0:T(8,128)(2,1)}, u32[]{:S(2)}) copy-start(bf16[128,256]{1,0:T(8,128)(2,1)} %constant.125.clone.thi_ref) | copy-start | bytes 196612
  0.0 27.4 %copy-start.22 = (f32[64,1,128]{2,1,0:T(1,128)S(1)}, f32[64,1,128]{2,1,0:T(1,128)}, u32[]{:S(2)}) copy-start(f32[64,1,128]{2,1,0:T(1,128)} %constant.124.clone.twi_ref) | copy-start | bytes 98308
  0.0 27.4 %copy-start.23 = (f32[64,1,128]{2,1,0:T(1,128)S(1)}, f32[64,1,128]{2,1,0:T(1,128)}, u32[]{:S(2)}) copy-start(f32[64,1,128]{2,1,0:T(1,128)} %constant.123.clone.twr_ref) | copy-start | bytes 98308
  0.0 27.4 %copy-start.26 = (bf16[16,256]{1,0:T(8,128)(2,1)S(1)}, bf16[16,256]{1,0:T(8,128)(2,1)}, u32[]{:S(2)}) copy-start(bf16[16,256]{1,0:T(8,128)(2,1)} %constant.127.clone.alt_ref) | copy-start | bytes 24580
  0.0 11.7 %copy-start.28 = (s32[1,64]{1,0:T(1,128)S(1)}, s32[1,64]{1,0:T(1,128)}, u32[]{:S(2)}) copy-start(s32[1,64]{1,0:T(1,128)} %param.30) | copy-start | bytes 772
  0.1 11.8 %copy-start.25 = (f32[2,2048]{1,0:T(2,128)S(1)}, f32[2,2048]{1,0:T(2,128)}, u32[]{:S(2)}) copy-start(f32[2,2048]{1,0:T(2,128)} %frac_ref.1) | copy-start | bytes 49156
  0.1 11.8 %copy-start.24 = (s32[2,2048]{1,0:T(2,128)S(1)}, s32[2,2048]{1,0:T(2,128)}, u32[]{:S(2)}) copy-start(s32[2,2048]{1,0:T(2,128)} %cell_ref.1) | copy-start | bytes 49156
  0.1 11.8 %copy-start.27 = (s32[2048]{0:T(1024)S(1)}, s32[2048]{0:T(1024)}, u32[]{:S(2)}) copy-start(s32[2048]{0:T(1024)} %param.31) | copy-start | bytes 24580
  4.2 23.2 %all-to-all-start = ((bf16[16,4,64,128]{3,2,1,0:T(8,128)(2,1)}), bf16[16,4,64,128]{3,2,1,0:T(8,128)(2,1)S(1)}, u32[]{:S(2)}, u32[]{:S(2)}) async-start(bf16[16,4,64,128]{3,2,1,0:T(8,128)(2,1)} %shard_map.271), calls=%async_computation | async-start | bytes 2097152 | tf_op jit(solution)/shard_map/all_to_all | solution.py:699
  27.5 36.7 %copy-start.2 = (bf16[256,256]{1,0:T(8,128)(2,1)S(1)}, bf16[256,256]{1,0:T(8,128)(2,1)}, u32[]{:S(2)}) copy-start(bf16[256,256]{1,0:T(8,128)(2,1)} %constant.135.clone.blo_ref) | copy-start | bytes 393220
  27.5 36.7 %copy-start.3 = (bf16[256,256]{1,0:T(8,128)(2,1)S(1)}, bf16[256,256]{1,0:T(8,128)(2,1)}, u32[]{:S(2)}) copy-start(bf16[256,256]{1,0:T(8,128)(2,1)} %constant.134.clone.bhi_ref) | copy-start | bytes 393220
  27.5 36.7 %copy-start.4 = (bf16[256,256]{1,0:T(8,128)(2,1)S(1)}, bf16[256,256]{1,0:T(8,128)(2,1)}, u32[]{:S(2)}) copy-start(bf16[256,256]{1,0:T(8,128)(2,1)} %constant.133.clone.flo_ref) | copy-start | bytes 393220
  27.5 36.7 %copy-start.5 = (bf16[256,256]{1,0:T(8,128)(2,1)S(1)}, bf16[256,256]{1,0:T(8,128)(2,1)}, u32[]{:S(2)}) copy-start(bf16[256,256]{1,0:T(8,128)(2,1)} %constant.132.clone.fhi_ref) | copy-start | bytes 393220
  27.5 36.7 %copy-start.12 = (f32[128,1,128]{2,1,0:T(1,128)S(1)}, f32[128,1,128]{2,1,0:T(1,128)}, u32[]{:S(2)}) copy-start(f32[128,1,128]{2,1,0:T(1,128)} %constant.139.clone.del_ref) | copy-start | bytes 196612
  27.5 36.7 %copy-start.13 = (f32[128,1,128]{2,1,0:T(1,128)S(1)}, f32[128,1,128]{2,1,0:T(1,128)}, u32[]{:S(2)}) copy-start(f32[128,1,128]{2,1,0:T(1,128)} %constant.138.clone.sm_ref) | copy-start | bytes 196612
  27.5 36.7 %copy-start.14 = (f32[128,1,128]{2,1,0:T(1,128)S(1)}, f32[128,1,128]{2,1,0:T(1,128)}, u32[]{:S(2)}) copy-start(f32[128,1,128]{2,1,0:T(1,128)} %constant.137.clone.pm_ref) | copy-start | bytes 196612
  27.6 36.7 %copy-start.15 = (f32[128,1,128]{2,1,0:T(1,128)S(1)}, f32[128,1,128]{2,1,0:T(1,128)}, u32[]{:S(2)}) copy-start(f32[128,1,128]{2,1,0:T(1,128)} %constant.136.clone.wm2_ref) | copy-start | bytes 196612
  27.6 36.7 %copy-start.16 = (f32[128,128]{1,0:T(8,128)S(1)}, f32[128,128]{1,0:T(8,128)}, u32[]{:S(2)}) copy-start(f32[128,128]{1,0:T(8,128)} %constant.131.clone.tw2i_ref) | copy-start | bytes 196612
  27.6 36.7 %copy-start.17 = (f32[128,128]{1,0:T(8,128)S(1)}, f32[128,128]{1,0:T(8,128)}, u32[]{:S(2)}) copy-start(f32[128,128]{1,0:T(8,128)} %constant.130.clone.tw2r_ref) | copy-start | bytes 196612
  33.6 30.6 %copy-start.18 = (f32[128,1,128]{2,1,0:T(1,128)S(1)}, f32[128,1,128]{2,1,0:T(1,128)}, u32[]{:S(2)}) copy-start(f32[128,1,128]{2,1,0:T(1,128)} %constant.129.clone.twi_ref) | copy-start | bytes 196612
  33.6 30.7 %copy-start.19 = (f32[128,1,128]{2,1,0:T(1,128)S(1)}, f32[128,1,128]{2,1,0:T(1,128)}, u32[]{:S(2)}) copy-start(f32[128,1,128]{2,1,0:T(1,128)} %constant.128.clone.twr_ref) | copy-start | bytes 196612
  33.6 30.6 %all-to-all-start.1 = ((bf16[128,40,128]{2,1,0:T(8,128)(2,1)}), bf16[128,40,128]{2,1,0:T(8,128)(2,1)S(1)}, u32[]{:S(2)}, u32[]{:S(2)}) async-start(bf16[128,40,128]{2,1,0:T(8,128)(2,1)} %shard_map.273), calls=%async_computation.1 | async-start | bytes 2621440 | tf_op jit(solution)/shard_map/all_to_all | solution.py:701
  77.6 34.4 %copy-start.1 = (bf16[256,256]{1,0:T(8,128)(2,1)S(1)}, bf16[256,256]{1,0:T(8,128)(2,1)}, u32[]{:S(2)}) copy-start(bf16[256,256]{1,0:T(8,128)(2,1)} %constant.140.clone.t_ref) | copy-start | bytes 393220
  77.6 34.4 %copy-start.7 = (f32[128,128]{1,0:T(8,128)S(1)}, f32[128,128]{1,0:T(8,128)}, u32[]{:S(2)}) copy-start(f32[128,128]{1,0:T(8,128)} %constant.145.clone.alt_ref) | copy-start | bytes 196612
  77.7 34.4 %copy-start.8 = (f32[128,128]{1,0:T(8,128)S(1)}, f32[128,128]{1,0:T(8,128)}, u32[]{:S(2)}) copy-start(f32[128,128]{1,0:T(8,128)} %constant.144.clone.omi_ref) | copy-start | bytes 196612
  77.7 34.3 %copy-start.9 = (f32[128,128]{1,0:T(8,128)S(1)}, f32[128,128]{1,0:T(8,128)}, u32[]{:S(2)}) copy-start(f32[128,128]{1,0:T(8,128)} %constant.143.clone.omr_ref) | copy-start | bytes 196612
  77.7 34.3 %copy-start.10 = (f32[128,128]{1,0:T(8,128)S(1)}, f32[128,128]{1,0:T(8,128)}, u32[]{:S(2)}) copy-start(f32[128,128]{1,0:T(8,128)} %constant.142.clone.t0i_ref) | copy-start | bytes 196612
  77.7 34.3 %copy-start.11 = (f32[128,128]{1,0:T(8,128)S(1)}, f32[128,128]{1,0:T(8,128)}, u32[]{:S(2)}) copy-start(f32[128,128]{1,0:T(8,128)} %constant.141.clone.t0r_ref) | copy-start | bytes 196612
  121.9 29.8 %all-to-all-start.3 = ((bf16[16,2,2,128,128]{4,3,2,1,0:T(8,128)(2,1)}), bf16[16,2,2,128,128]{4,3,2,1,0:T(8,128)(2,1)S(1)}, u32[]{:S(2)}, u32[]{:S(2)}) async-start(bf16[16,2,2,128,128]{4,3,2,1,0:T(8,128)(2,1)} %shard_map.275), calls=%async_computation.3 | async-start | bytes 4194304 | tf_op jit(solution)/shard_map/all_to_all | solution.py:705
  151.7 1.0 copy-start
